TPU v7x, 32 devices: a whole 2x2x4 slice. The times are simulated.
32 devices in a mesh: gx: 4 (over z), gz: 4 (over y, x), gy: 2 (over core).
Axes of the slice: x: 2, y: 2, z: 4, core: 2. Of those that a mesh axis runs over, the one named last changes fastest.
Arguments:
- row_embed: bfloat16 [65536, 128], P(('gx', 'gz')), may hold values from -24 to 24, as said below
- col_embed: bfloat16 [1024, 128], P('gy'), may hold values from -24 to 24, as said below
- row_mass: float32 [65536], P(('gx', 'gz')), may hold values from 1 to 10
- col_mass: float32 [1024], P('gy'), may hold values from 1 to 10
Outputs:
- row_potential: float32 [65536], P(('gx', 'gz'))
- col_potential: float32 [1024], P('gy')
- errors: float32 [10, 2], replicated
Inputs may be any that keep to these rules, and one draw needn't show every extreme that they name: `row_embed`: entries are real-valued embedding coordinates. `col_embed`: entries are real-valued embedding coordinates.
All inputs are finite; a program needn't handle non-finite values.
Results may differ from a plain program's by a relative error of at most 0.0003.
Values sent between devices are 32-bit elements; how exact they have to be, the bound alone decides.
A program may use at most 64 MiB of HBM per device.

v0:
```python
import functools
import math

import jax
import jax.numpy as jnp
from jax import lax
from jax.experimental import pallas as pl
from jax.experimental.pallas import tpu as pltpu
from jax.sharding import PartitionSpec as P

ITERS = 10
eps = 0.05
LANES = 128
CHUNK = 8
SUB = 32
PAIR = 4
PERIOD = 3
SHIFT = 40.0
SCALE = math.log2(math.e) / eps
F32 = jnp.float32
MESH = pl.DeviceIdType.MESH


def kernel(nx, nz, ny, x_hbm, y_hbm, rm_hbm, cm_hbm, f_out, g_out, e_out,
           m_ref, t_ref, gb_ref, acc_ref, f_ref, w_ref, a_ref, rho_ref, cap_ref, gc_ref, b_ref,
           err0_ref, errmat, u_ref, v_ref, lse_ref, rbuf0, rbuf, cbuf0, cbuf, ebuf,
           x_ref, y_ref, rm_ref, cm_ref, s_x, s_y, s_m, s_r0, r_r0, s_r, r_r, s_c0, r_c0, s_c, r_c, s_e, r_e):
    rows, width = x_ref.shape
    cols = y_ref.shape[0]
    tiles = rows // LANES
    ctiles = cols // LANES
    chunks = tiles // CHUNK
    nsub = cols // SUB
    ix, iz, iy = lax.axis_index("gx"), lax.axis_index("gz"), lax.axis_index("gy")
    ng = nx * nz
    me = ix * nz + iz

    def col_peer(d):
        other = lax.rem(me + d, ng)
        return {"gx": other // nz, "gz": lax.rem(other, nz)}

    def row_peer(d):
        return {"gy": lax.rem(iy + d, ny)}

    barrier = pltpu.get_barrier_semaphore()
    for d in range(1, ng):
        pl.semaphore_signal(barrier, inc=1, device_id=col_peer(d), device_id_type=MESH)
    for d in range(1, ny):
        pl.semaphore_signal(barrier, inc=1, device_id=row_peer(d), device_id_type=MESH)

    y_copy = pltpu.make_async_copy(y_hbm, y_ref, s_y)
    y_copy.start()
    half = rows // 2
    x_copies = [pltpu.make_async_copy(x_hbm.at[pl.ds(h * half, half)], x_ref.at[pl.ds(h * half, half)], s_x.at[h])
                for h in range(2)]
    m_copies = [pltpu.make_async_copy(cm_hbm, cm_ref, s_m.at[0]), pltpu.make_async_copy(rm_hbm, rm_ref, s_m.at[1])]
    for copy in x_copies + m_copies:
        copy.start()

    def send(buf, ssem, rsem, peers):
        for peer in peers:
            pltpu.make_async_remote_copy(
                src_ref=buf, dst_ref=buf, send_sem=ssem, recv_sem=rsem,
                device_id=peer, device_id_type=MESH).start()

    def drain(some, sem):
        pltpu.make_async_copy(some, some, sem).wait()

    def flip(p, bit):
        return p + bit - 2 * bit * lax.rem(p // bit, 2)

    def far_peer(i):
        px, pz = ix, iz
        for step in range(ng.bit_length()):
            bit = 1 << step
            if (i // nz) & bit:
                px = flip(px, bit)
            if (i % nz) & bit:
                pz = flip(pz, bit)
        return {"gx": px, "gz": pz}

    if nx & (nx - 1) or nz & (nz - 1):
        col_peers = [col_peer(d) for d in range(1, ng)]
    else:
        col_peers = [far_peer(i) for i in range(ng - 1, 0, -1)]
    row_peers = [row_peer(d) for d in range(1, ny)]

    def spread(compact):
        for t in range(ctiles):
            block = jnp.broadcast_to(compact[t:t + 1, :], (LANES, LANES))
            gb_ref[t * LANES:(t + 1) * LANES, :] = jnp.transpose(block)

    def squeeze(ref, op):
        return jnp.concatenate(
            [op(jnp.transpose(ref[t * LANES:(t + 1) * LANES, :]), axis=0, keepdims=True)
             for t in range(ctiles)], axis=0)

    factor = 2.0 * SCALE / width
    ones = jnp.ones((8, width), jnp.bfloat16)
    nt = (((1,), (1,)), ((), ()))
    group = math.gcd(CHUNK, 4)

    def fold(v, op):
        out = v[0:8]
        for q in range(1, v.shape[0] // 8):
            out = op(out, v[q * 8:(q + 1) * 8])
        return out

    def row_norm(v):
        square = v * v
        high = square.astype(jnp.bfloat16)
        low = (square - high.astype(F32)).astype(jnp.bfloat16)
        parts = [lax.dot_general(ones, part, nt, preferred_element_type=F32) for part in (high, low)]
        return (parts[0] + parts[1]) * (SCALE / width)

    y_copy.wait()
    yv = y_ref[...]
    yf = yv.astype(F32)
    ysq = row_norm(yf)
    kap = jnp.concatenate([ysq[0:1, t * LANES:(t + 1) * LANES] for t in range(ctiles)], axis=0)
    cap_ref[...] = kap
    spread(-kap)
    for copy in m_copies:
        copy.wait()
    csum = jnp.broadcast_to(jnp.sum(cm_ref[...], axis=0, keepdims=True), (CHUNK, LANES))
    for c in range(chunks):
        rbuf0[c, iy, 2 * CHUNK:3 * CHUNK, :] = csum

    def build(i, carry):
        xb = x_ref[pl.ds(pl.multiple_of(i * group * LANES, group * LANES), group * LANES), :]
        prod = lax.dot_general(y_ref[...], xb, nt, preferred_element_type=F32) * factor
        for q in range(group):
            m_ref[i * group + q] = prod[:, q * LANES:(q + 1) * LANES]
        tops = [None] * group
        for s in range(nsub):
            sl = slice(s * SUB, (s + 1) * SUB)
            gv = gb_ref[sl, :]
            for q in range(group):
                part = fold(m_ref[i * group + q, sl, :] + gv, jnp.maximum)
                tops[q] = part if tops[q] is None else jnp.maximum(tops[q], part)
        tops = [jnp.max(top, axis=0, keepdims=True) for top in tops]
        tots = [jnp.zeros((8, LANES), F32) for q in range(group)]
        for s in range(nsub):
            sl = slice(s * SUB, (s + 1) * SUB)
            gv = gb_ref[sl, :]
            for q in range(group):
                val = jnp.exp2((m_ref[i * group + q, sl, :] + gv) - tops[q])
                tots[q] = tots[q] + fold(val, jnp.add)
        c = i * group // CHUNK
        for q in range(group):
            at = lax.rem(i * group, CHUNK) + q
            rbuf0[c, iy, pl.ds(at, 1), :] = tops[q]
            rbuf0[c, iy, pl.ds(CHUNK + at, 1), :] = jnp.sum(tots[q], axis=0, keepdims=True)
        return carry

    per = CHUNK // group
    halfway = chunks // 2
    x_copies[0].wait()

    def build_chunk(c, carry):
        lax.fori_loop(c * per, (c + 1) * per, build, 0)
        return carry

    lax.fori_loop(0, halfway, build_chunk, 0)
    x_copies[1].wait()
    pl.semaphore_wait(barrier, (ng - 1) + (ny - 1))

    def push0(c, carry):
        send(rbuf0.at[c, iy], s_r0.at[c], r_r0.at[c], row_peers)
        return carry

    lax.fori_loop(0, halfway, push0, 0)

    def build_push(c, carry):
        build_chunk(c, 0)
        return push0(c, 0)

    lax.fori_loop(halfway, chunks, build_push, 0)
    acc_ref[...] = jnp.full((cols, LANES), -jnp.inf, F32)

    def colmax(c, carry):
        drain(rbuf0.at[c, 0:ny - 1], r_r0.at[c])
        drain(rbuf0.at[c, 0:ny - 1], s_r0.at[c])
        top = rbuf0[c, 0, 0:CHUNK, :]
        for d in range(1, ny):
            top = jnp.maximum(top, rbuf0[c, d, 0:CHUNK, :])
        tot = jnp.zeros((CHUNK, LANES), F32)
        for d in range(ny):
            tot = tot + rbuf0[c, d, CHUNK:2 * CHUNK, :] * jnp.exp2(rbuf0[c, d, 0:CHUNK, :] - top)
        lse = top + jnp.log2(tot)
        sl8 = pl.ds(pl.multiple_of(c * CHUNK, CHUNK), CHUNK)
        lse_ref[sl8, :] = lse
        fv = jnp.log2(rm_ref[sl8, :]) - lse
        f_ref[sl8, :] = fv
        w_ref[...] = fv
        for s in range(nsub):
            sl = slice(s * SUB, (s + 1) * SUB)
            acc = acc_ref[sl, :]
            for q in range(CHUNK):
                acc = jnp.maximum(acc, m_ref[c * CHUNK + q, sl, :] + w_ref[q:q + 1, :])
            acc_ref[sl, :] = acc
        return carry

    lax.fori_loop(0, chunks, colmax, 0)
    ctop = squeeze(acc_ref, jnp.max)
    spread(ctop)
    acc_ref[...] = jnp.zeros((cols, LANES), F32)

    def colsum(c, carry):
        w_ref[...] = f_ref[pl.ds(pl.multiple_of(c * CHUNK, CHUNK), CHUNK), :]
        for s in range(nsub):
            sl = slice(s * SUB, (s + 1) * SUB)
            acc = acc_ref[sl, :]
            gv = gb_ref[sl, :]
            for q in range(CHUNK):
                acc = acc + jnp.exp2((m_ref[c * CHUNK + q, sl, :] + w_ref[q:q + 1, :]) - gv)
            acc_ref[sl, :] = acc
        return carry

    lax.fori_loop(0, chunks, colsum, 0)
    ctot = rbuf0[0, 0, 2 * CHUNK:2 * CHUNK + 1, :]
    for d in range(1, ny):
        ctot = ctot + rbuf0[0, d, 2 * CHUNK:2 * CHUNK + 1, :]
    b_ref[...] = cm_ref[...] / jnp.sum(ctot, axis=1, keepdims=True)
    mass = rm_ref[...]
    lse = lse_ref[...]
    cbuf0[me, 0:ctiles, :] = ctop
    cbuf0[me, ctiles:2 * ctiles, :] = squeeze(acc_ref, jnp.sum)
    cbuf0[me, 2 * ctiles:2 * ctiles + 1, :] = jnp.sum(mass, axis=0, keepdims=True)
    send(cbuf0.at[me], s_c0, r_c0, col_peers)

    def norms(i, carry):
        xf = x_ref[pl.ds(pl.multiple_of(i * group * LANES, group * LANES), group * LANES), :].astype(F32)
        sq = row_norm(xf)
        for q in range(group):
            rho_ref[pl.ds(i * group + q, 1), :] = sq[0:1, q * LANES:(q + 1) * LANES]
        return carry

    lax.fori_loop(0, tiles // group, norms, 0)
    drain(cbuf0.at[0:ng - 1], r_c0)
    drain(cbuf0.at[0:ng - 1], s_c0)
    top = cbuf0[0, 0:ctiles, :]
    rtot = cbuf0[0, 2 * ctiles:2 * ctiles + 1, :]
    for d in range(1, ng):
        top = jnp.maximum(top, cbuf0[d, 0:ctiles, :])
        rtot = rtot + cbuf0[d, 2 * ctiles:2 * ctiles + 1, :]
    tot = jnp.zeros((ctiles, LANES), F32)
    for d in range(ng):
        tot = tot + cbuf0[d, ctiles:2 * ctiles, :] * jnp.exp2(cbuf0[d, 0:ctiles, :] - top)
    rtot = jnp.sum(rtot, axis=1, keepdims=True)
    lrt = jnp.log2(rtot)
    a = mass / rtot
    a_ref[...] = a
    f_ref[...] = f_ref[...] - lrt
    err0_ref[...] = jnp.sum(jnp.abs(jnp.exp2(lse - rho_ref[...]) - a), axis=0, keepdims=True)
    clse = top + jnp.log2(tot) - lrt
    bv = b_ref[...]
    gc = jnp.log2(bv) - clse
    gc_ref[...] = gc
    spread(gc)
    lane = lax.broadcasted_iota(jnp.int32, (1, LANES), 1)
    errmat[...] = jnp.zeros_like(errmat)
    ebuf[iy] = jnp.zeros(ebuf.shape[1:], F32)
    ebuf[iy, 0:1, :] = jnp.sum(jnp.abs(jnp.exp2(clse - cap_ref[...]) - bv), axis=0, keepdims=True)

    def iteration(k, phase):
        par = lax.rem(k, 2)

        def row_chunk(c, carry):
            for q0 in range(0, CHUNK, PAIR):
                tots = [jnp.zeros((8, LANES), F32) for q in range(PAIR)]
                if phase == 0:
                    fvs = [f_ref[pl.ds(c * CHUNK + q0 + q, 1), :] + SHIFT for q in range(PAIR)]
                for s in range(nsub):
                    sl = slice(s * SUB, (s + 1) * SUB)
                    gv = gb_ref[sl, :]
                    for q in range(PAIR):
                        t = c * CHUNK + q0 + q
                        if phase == 0:
                            val = jnp.exp2((m_ref[t, sl, :] + gv) + fvs[q])
                            t_ref[t, sl, :] = val
                        else:
                            val = t_ref[t, sl, :] * gv
                        tots[q] = tots[q] + fold(val, jnp.add)
                for q in range(PAIR):
                    rbuf[par, c, iy, q0 + q:q0 + q + 1, :] = jnp.sum(tots[q], axis=0, keepdims=True)
            send(rbuf.at[par, c, iy], s_r.at[par, c], r_r.at[par, c], row_peers)
            return carry

        lax.fori_loop(0, chunks, row_chunk, 0, unroll=True)
        acc_ref[...] = jnp.zeros((cols, LANES), F32)

        def col_chunk(c, err):
            drain(rbuf.at[par, c, 0:ny - 1], r_r.at[par, c])
            drain(rbuf.at[par, c, 0:ny - 1], s_r.at[par, c])
            r = rbuf[par, c, 0]
            for d in range(1, ny):
                r = r + rbuf[par, c, d]
            r = r * 2.0 ** -SHIFT
            sl8 = pl.ds(pl.multiple_of(c * CHUNK, CHUNK), CHUNK)
            av = a_ref[sl8, :]
            old = r if phase == 0 else r * u_ref[sl8, :]
            u = av / r
            u_ref[sl8, :] = u
            w_ref[...] = u
            err = err + jnp.sum(jnp.abs(old - av), axis=0, keepdims=True)
            for s in range(nsub):
                sl = slice(s * SUB, (s + 1) * SUB)
                acc = acc_ref[sl, :]
                for q in range(CHUNK):
                    acc = acc + t_ref[c * CHUNK + q, sl, :] * w_ref[q:q + 1, :]
                acc_ref[sl, :] = acc
            return err

        err = lax.fori_loop(0, chunks, col_chunk, jnp.zeros((1, LANES), F32))
        cbuf[par, me, 0:ctiles, :] = squeeze(acc_ref, jnp.sum)
        cbuf[par, me, ctiles:ctiles + 1, :] = err
        cbuf[par, me, ctiles + 1:ctiles + 2, :] = err0_ref[...]
        send(cbuf.at[par, me, 0:ctiles + 2], s_c.at[par], r_c.at[par], col_peers)
        if phase == PERIOD - 1:
            f_ref[...] = f_ref[...] + jnp.log2(u_ref[...])
        drain(cbuf.at[par, 0:ng - 1, 0:ctiles + 2], r_c.at[par])
        got = cbuf[par, 0]
        for d in range(1, ng):
            got = got + cbuf[par, d]
        s = got[0:ctiles] * 2.0 ** -SHIFT
        bv = b_ref[...]
        v = bv / s
        if phase == PERIOD - 1:
            gc = gc_ref[...] + jnp.log2(v)
            gc_ref[...] = gc
            spread(gc)
        else:
            spread(v)
        old = s if phase == 0 else s * v_ref[...]
        v_ref[...] = v
        drain(cbuf.at[par, 0:ng - 1, 0:ctiles + 2], s_c.at[par])
        ebuf[iy, pl.ds(k, 1), :] = jnp.sum(jnp.abs(old - bv), axis=0, keepdims=True)
        rerr = jnp.sum(got[ctiles:ctiles + 2], axis=1, keepdims=True)
        errmat[pl.ds(k, 1), :] = jnp.broadcast_to(rerr[0:1], (1, LANES))
        errmat[0:1, :] = jnp.broadcast_to(rerr[1:2], (1, LANES))

    def period(j, carry):
        for phase in range(PERIOD):
            iteration(1 + j * PERIOD + phase, phase)
        return carry

    lax.fori_loop(0, (ITERS - 1) // PERIOD, period, 0)
    send(ebuf.at[iy], s_e, r_e, row_peers)
    f_out[...] = (f_ref[...] + rho_ref[...]) * (1.0 / SCALE)
    g_out[...] = (gc_ref[...] + cap_ref[...]) * (1.0 / SCALE)
    drain(ebuf.at[0:ny - 1], r_e)
    drain(ebuf.at[0:ny - 1], s_e)
    ce = ebuf[0]
    for d in range(1, ny):
        ce = ce + ebuf[d]
    ce = jnp.sum(ce, axis=1, keepdims=True)
    both = jnp.where(lane == 0, errmat[...], ce)
    e_out[...] = both[0:ITERS, 0:2]


def on_device(row_embed, col_embed, row_mass, col_mass):
    rows, width = row_embed.shape
    cols = col_embed.shape[0]
    nx, nz, ny = lax.axis_size("gx"), lax.axis_size("gz"), lax.axis_size("gy")
    ng = nx * nz
    tiles, ctiles = rows // LANES, cols // LANES
    chunks = tiles // CHUNK
    pad = -(-ITERS // 8) * 8
    crow0 = -(-(2 * ctiles + 1) // 8) * 8
    crow = -(-(ctiles + 2) // 8) * 8
    vm = lambda *s: pltpu.VMEM(s, F32)
    dma = pltpu.SemaphoreType.DMA
    f, g, e = pl.pallas_call(
        functools.partial(kernel, nx, nz, ny),
        out_shape=(jax.ShapeDtypeStruct((tiles, LANES), F32),
                   jax.ShapeDtypeStruct((ctiles, LANES), F32),
                   jax.ShapeDtypeStruct((ITERS, 2), F32)),
        in_specs=[pl.BlockSpec(memory_space=pl.ANY)] * 4,
        out_specs=[pl.BlockSpec(memory_space=pltpu.VMEM)] * 3,
        scratch_shapes=[
            vm(tiles, cols, LANES), vm(tiles, cols, LANES), vm(cols, LANES), vm(cols, LANES),
            vm(tiles, LANES), vm(CHUNK, LANES), vm(tiles, LANES), vm(tiles, LANES),
            vm(ctiles, LANES), vm(ctiles, LANES), vm(ctiles, LANES),
            vm(1, LANES), vm(pad, LANES), vm(tiles, LANES), vm(ctiles, LANES),
            vm(tiles, LANES), vm(chunks, ny, 3 * CHUNK, LANES), vm(2, chunks, ny, CHUNK, LANES),
            vm(ng, crow0, LANES), vm(2, ng, crow, LANES), vm(ny, pad, LANES),
            pltpu.VMEM((rows, width), row_embed.dtype), pltpu.VMEM((cols, width), col_embed.dtype),
            vm(tiles, LANES), vm(ctiles, LANES), dma((2,)), dma, dma((2,)), dma((chunks,)), dma((chunks,)), dma((2, chunks)), dma((2, chunks)), dma, dma, dma((2,)), dma((2,)), dma, dma,
        ],
        compiler_params=pltpu.CompilerParams(
            collective_id=0, has_side_effects=True, vmem_limit_bytes=67043328),
    )(row_embed, col_embed, row_mass.reshape(tiles, LANES), col_mass.reshape(ctiles, LANES))
    return f.reshape(rows), g.reshape(cols), e


def solution(mesh):
    in_specs = (P(("gx", "gz"), None), P("gy", None), P(("gx", "gz")), P("gy"))
    out_specs = (P(("gx", "gz")), P("gy"), P())
    return jax.shard_map(
        on_device, mesh=mesh, in_specs=in_specs, out_specs=out_specs, check_vma=False
    )
```

profile of v0, /device:TPU:0, one launch (start us, length us, event | category | flops | bytes accessed | tf_op | source)
XLA Modules:
  0.0 81.2 jit_solution(6772511436238976994)
XLA Ops:
  0.6 78.0 %shard_map.67 = (f32[32,128]{1,0:T(8,128)}, f32[4,128]{1,0:T(4,128)}, f32[10,2]{1,0:T(8,128)}) custom-call(bf16[4096,128]{1,0:T(8,128)(2,1)} %x_hbm.1, bf16[512,128]{1,0:T(8,128)(2,1)} %y_hbm.1, f32[32,128]{1,0:T(8,128)} %bitcast.4, f32[4,128]{1,0:T(4,128)} %bitcast.6), custom_call_target="tpu_custom_call" | custom-call | tf_op jit(solution)/shard_map/pallas_call | solution.py:374
  78.6 0.0 copy-start
  78.7 1.3 %copy.7 = f32[10,2]{0,1:T(2,128)} copy(f32[10,2]{1,0:T(8,128)} %get-tuple-element.11) | data formatting | bytes 160
  80.0 0.0 copy-done
  80.0 0.0 copy-start.1
  80.0 0.6 copy.10
  80.6 0.1 copy-done.1
  80.7 0.6 copy.11
Async XLA Ops:
  78.6 1.4 %copy-start = (f32[32,128]{1,0:T(8,128)S(1)}, f32[32,128]{1,0:T(8,128)}, u32[]{:S(2)}) copy-start(f32[32,128]{1,0:T(8,128)} %get-tuple-element.6) | copy-start | bytes 49156
  80.0 0.7 copy-start.1
where the time goes:
time: 81.5 us; the launch traced here: 81.2 us
  Pallas kernels  78 us (96%)
  local copies, waits for them, and re-layouts  2.59 us (3%)
    pallas_call x1, Pallas kernels, on_device(): pl.pallas_call(functools.partial(kernel, nx, nz, ny), out_shape=(jax.Shap...  78 us
    unnamed x7, local copies, waits for them, and re-layouts  2.59 us

commit v1 on v0

v1 whole, which is shorter than its diff:
```python
import functools
import math

import jax
import jax.numpy as jnp
from jax import lax
from jax.experimental import pallas as pl
from jax.experimental.pallas import tpu as pltpu
from jax.sharding import PartitionSpec as P

ITERS = 10
eps = 0.05
LANES = 128
CHUNK = 8
SUB = 32
SCALE = math.log2(math.e) / eps
F32 = jnp.float32
MESH = pl.DeviceIdType.MESH


def kernel(nx, nz, ny, x_hbm, y_hbm, rm_hbm, cm_hbm, f_out, g_out, e_out,
           m_ref, t_ref, f_ref, r_ref, a_ref, rho_ref, cap_ref, gc_ref, b_ref,
           err0_ref, errs_ref, w_ref, v_ref, lse_ref, rbuf0, rbuf, cbuf0, cbuf, ebuf,
           x_ref, y_ref, rm_ref, cm_ref, s_x, s_y, s_m, s_r0, r_r0, s_r, r_r, s_c0, r_c0, s_c, r_c, s_e, r_e):
    rows, width = x_ref.shape
    cols = y_ref.shape[0]
    tiles = rows // LANES
    ctiles = cols // LANES
    chunks = tiles // CHUNK
    nsub = cols // SUB
    gb, ga, gl, gu = range(tiles, tiles + 4)
    ix, iz, iy = lax.axis_index("gx"), lax.axis_index("gz"), lax.axis_index("gy")
    ng = nx * nz
    me = ix * nz + iz
    pad = ebuf.shape[1]

    def col_peer(d):
        other = lax.rem(me + d, ng)
        return {"gx": other // nz, "gz": lax.rem(other, nz)}

    def row_peer(d):
        return {"gy": lax.rem(iy + d, ny)}

    barrier = pltpu.get_barrier_semaphore()
    for d in range(1, ng):
        pl.semaphore_signal(barrier, inc=1, device_id=col_peer(d), device_id_type=MESH)
    for d in range(1, ny):
        pl.semaphore_signal(barrier, inc=1, device_id=row_peer(d), device_id_type=MESH)

    y_copy = pltpu.make_async_copy(y_hbm, y_ref, s_y)
    y_copy.start()
    half = rows // 2
    x_copies = [pltpu.make_async_copy(x_hbm.at[pl.ds(h * half, half)], x_ref.at[pl.ds(h * half, half)], s_x.at[h])
                for h in range(2)]
    m_copies = [pltpu.make_async_copy(cm_hbm, cm_ref, s_m.at[0]), pltpu.make_async_copy(rm_hbm, rm_ref, s_m.at[1])]
    for copy in x_copies + m_copies:
        copy.start()

    def send(buf, ssem, rsem, peers):
        for peer in peers:
            pltpu.make_async_remote_copy(
                src_ref=buf, dst_ref=buf, send_sem=ssem, recv_sem=rsem,
                device_id=peer, device_id_type=MESH).start()

    def drain(some, sem):
        pltpu.make_async_copy(some, some, sem).wait()

    def flip(p, bit):
        return p + bit - 2 * bit * lax.rem(p // bit, 2)

    def far_peer(i):
        px, pz = ix, iz
        for step in range(ng.bit_length()):
            bit = 1 << step
            if (i // nz) & bit:
                px = flip(px, bit)
            if (i % nz) & bit:
                pz = flip(pz, bit)
        return {"gx": px, "gz": pz}

    if nx & (nx - 1) or nz & (nz - 1):
        col_peers = [col_peer(d) for d in range(1, ng)]
    else:
        col_peers = [far_peer(i) for i in range(ng - 1, 0, -1)]
    row_peers = [row_peer(d) for d in range(1, ny)]

    def spread(compact, slot):
        for t in range(ctiles):
            block = jnp.broadcast_to(compact[t:t + 1, :], (LANES, LANES))
            t_ref[slot, t * LANES:(t + 1) * LANES, :] = jnp.transpose(block)

    def squeeze(op):
        return jnp.concatenate(
            [op(jnp.transpose(t_ref[ga, t * LANES:(t + 1) * LANES, :]), axis=0, keepdims=True)
             for t in range(ctiles)], axis=0)

    factor = 2.0 * SCALE / width
    ones = jnp.ones((8, width), jnp.bfloat16)
    nt = (((1,), (1,)), ((), ()))
    group = math.gcd(CHUNK, 4)

    def fold(v, op):
        out = v[0:8]
        for q in range(1, v.shape[0] // 8):
            out = op(out, v[q * 8:(q + 1) * 8])
        return out

    def row_norm(v):
        square = v * v
        high = square.astype(jnp.bfloat16)
        low = (square - high.astype(F32)).astype(jnp.bfloat16)
        parts = [lax.dot_general(ones, part, nt, preferred_element_type=F32) for part in (high, low)]
        return (parts[0] + parts[1]) * (SCALE / width)

    y_copy.wait()
    yv = y_ref[...]
    yf = yv.astype(F32)
    ysq = row_norm(yf)
    kap = jnp.concatenate([ysq[0:1, t * LANES:(t + 1) * LANES] for t in range(ctiles)], axis=0)
    cap_ref[...] = kap
    spread(-kap, gb)
    for copy in m_copies:
        copy.wait()
    csum = jnp.broadcast_to(jnp.sum(cm_ref[...], axis=0, keepdims=True), (CHUNK, LANES))
    for c in range(chunks):
        rbuf0[c, iy, 2 * CHUNK:3 * CHUNK, :] = csum

    def build(i, carry):
        xb = x_ref[pl.ds(pl.multiple_of(i * group * LANES, group * LANES), group * LANES), :]
        prod = lax.dot_general(y_ref[...], xb, nt, preferred_element_type=F32) * factor
        for q in range(group):
            m_ref[i * group + q] = prod[:, q * LANES:(q + 1) * LANES]
        tops = [None] * group
        for s in range(nsub):
            sl = slice(s * SUB, (s + 1) * SUB)
            gv = t_ref[gb, sl, :]
            for q in range(group):
                part = fold(m_ref[i * group + q, sl, :] + gv, jnp.maximum)
                tops[q] = part if tops[q] is None else jnp.maximum(tops[q], part)
        tops = [jnp.max(top, axis=0, keepdims=True) for top in tops]
        tots = [jnp.zeros((8, LANES), F32) for q in range(group)]
        for s in range(nsub):
            sl = slice(s * SUB, (s + 1) * SUB)
            gv = t_ref[gb, sl, :]
            for q in range(group):
                val = jnp.exp2((m_ref[i * group + q, sl, :] + gv) - tops[q])
                tots[q] = tots[q] + fold(val, jnp.add)
        c = i * group // CHUNK
        for q in range(group):
            at = lax.rem(i * group, CHUNK) + q
            rbuf0[c, iy, pl.ds(at, 1), :] = tops[q]
            rbuf0[c, iy, pl.ds(CHUNK + at, 1), :] = jnp.sum(tots[q], axis=0, keepdims=True)
        return carry

    steps = tiles // group
    x_copies[0].wait()
    lax.fori_loop(0, steps // 2, build, 0)
    x_copies[1].wait()
    lax.fori_loop(steps // 2, steps, build, 0)
    pl.semaphore_wait(barrier, (ng - 1) + (ny - 1))

    def push0(c, carry):
        send(rbuf0.at[c, iy], s_r0.at[c], r_r0.at[c], row_peers)
        return carry

    lax.fori_loop(0, chunks, push0, 0)
    t_ref[ga] = jnp.full((cols, LANES), -jnp.inf, F32)

    def colmax(c, carry):
        drain(rbuf0.at[c, 0:ny - 1], r_r0.at[c])
        drain(rbuf0.at[c, 0:ny - 1], s_r0.at[c])
        top = rbuf0[c, 0, 0:CHUNK, :]
        for d in range(1, ny):
            top = jnp.maximum(top, rbuf0[c, d, 0:CHUNK, :])
        tot = jnp.zeros((CHUNK, LANES), F32)
        for d in range(ny):
            tot = tot + rbuf0[c, d, CHUNK:2 * CHUNK, :] * jnp.exp2(rbuf0[c, d, 0:CHUNK, :] - top)
        lse = top + jnp.log2(tot)
        sl8 = pl.ds(pl.multiple_of(c * CHUNK, CHUNK), CHUNK)
        lse_ref[sl8, :] = lse
        fv = jnp.log2(rm_ref[sl8, :]) - lse
        f_ref[sl8, :] = fv
        w_ref[...] = fv
        for s in range(nsub):
            sl = slice(s * SUB, (s + 1) * SUB)
            acc = t_ref[ga, sl, :]
            for q in range(CHUNK):
                acc = jnp.maximum(acc, m_ref[c * CHUNK + q, sl, :] + w_ref[q:q + 1, :])
            t_ref[ga, sl, :] = acc
        return carry

    lax.fori_loop(0, chunks, colmax, 0)
    ctop = squeeze(jnp.max)
    spread(ctop, gb)
    t_ref[ga] = jnp.zeros((cols, LANES), F32)

    def colsum(c, carry):
        w_ref[...] = f_ref[pl.ds(pl.multiple_of(c * CHUNK, CHUNK), CHUNK), :]
        for s in range(nsub):
            sl = slice(s * SUB, (s + 1) * SUB)
            acc = t_ref[ga, sl, :]
            gv = t_ref[gb, sl, :]
            for q in range(CHUNK):
                val = jnp.exp2((m_ref[c * CHUNK + q, sl, :] + w_ref[q:q + 1, :]) - gv)
                t_ref[c * CHUNK + q, sl, :] = val
                acc = acc + val
            t_ref[ga, sl, :] = acc
        return carry

    lax.fori_loop(0, chunks, colsum, 0)
    ctot = rbuf0[0, 0, 2 * CHUNK:2 * CHUNK + 1, :]
    for d in range(1, ny):
        ctot = ctot + rbuf0[0, d, 2 * CHUNK:2 * CHUNK + 1, :]
    mass = rm_ref[...]
    cbuf0[me, 0:ctiles, :] = ctop
    cbuf0[me, ctiles:2 * ctiles, :] = squeeze(jnp.sum)
    cbuf0[me, 2 * ctiles:2 * ctiles + 1, :] = jnp.sum(mass, axis=0, keepdims=True)
    send(cbuf0.at[me], s_c0, r_c0, col_peers)
    b_ref[...] = cm_ref[...] / jnp.sum(ctot, axis=1, keepdims=True)

    def norms(i, carry):
        xf = x_ref[pl.ds(pl.multiple_of(i * group * LANES, group * LANES), group * LANES), :].astype(F32)
        sq = row_norm(xf)
        for q in range(group):
            rho_ref[pl.ds(i * group + q, 1), :] = sq[0:1, q * LANES:(q + 1) * LANES]
        return carry

    lax.fori_loop(0, tiles // group, norms, 0)
    errs_ref[...] = jnp.zeros_like(errs_ref)
    ebuf[iy] = jnp.zeros(ebuf.shape[1:], F32)
    drain(cbuf0.at[0:ng - 1], r_c0)
    top = cbuf0[0, 0:ctiles, :]
    rtot = cbuf0[0, 2 * ctiles:2 * ctiles + 1, :]
    for d in range(1, ng):
        top = jnp.maximum(top, cbuf0[d, 0:ctiles, :])
        rtot = rtot + cbuf0[d, 2 * ctiles:2 * ctiles + 1, :]
    tot = jnp.zeros((ctiles, LANES), F32)
    for d in range(ng):
        tot = tot + cbuf0[d, ctiles:2 * ctiles, :] * jnp.exp2(cbuf0[d, 0:ctiles, :] - top)
    bv = b_ref[...]
    v_ref[...] = bv * jnp.exp2(cbuf0[me, 0:ctiles, :] - top) / tot
    rtot = jnp.sum(rtot, axis=1, keepdims=True)
    lrt = jnp.log2(rtot)
    a = rm_ref[...] / rtot
    a_ref[...] = a
    f_ref[...] = f_ref[...] - lrt
    err0_ref[...] = jnp.sum(jnp.abs(jnp.exp2(lse_ref[...] - rho_ref[...]) - a), axis=0, keepdims=True)
    clse = top + jnp.log2(tot) - lrt
    gc_ref[...] = jnp.log2(bv) - clse
    ebuf[iy, 0:1, :] = jnp.sum(jnp.abs(jnp.exp2(clse - cap_ref[...]) - bv), axis=0, keepdims=True)
    drain(cbuf0.at[0:ng - 1], s_c0)

    def rebuild(i, carry):
        fvs = [f_ref[pl.ds(i * group + q, 1), :] for q in range(group)]
        for s in range(nsub):
            sl = slice(s * SUB, (s + 1) * SUB)
            gv = t_ref[gl, sl, :]
            for q in range(group):
                t_ref[i * group + q, sl, :] = jnp.exp2((m_ref[i * group + q, sl, :] + gv) + fvs[q])
        return carry

    def iteration(k, carry):
        par = lax.rem(k, 2)
        spread(v_ref[...], gb)
        for c in range(chunks):
            tots = [None] * CHUNK
            for s in range(nsub):
                sl = slice(s * SUB, (s + 1) * SUB)
                gv = t_ref[gb, sl, :]
                for q in range(CHUNK):
                    part = fold(t_ref[c * CHUNK + q, sl, :] * gv, jnp.add)
                    tots[q] = part if tots[q] is None else tots[q] + part
            for q in range(CHUNK):
                rbuf[par, c, iy, q:q + 1, :] = jnp.sum(tots[q], axis=0, keepdims=True)
            send(rbuf.at[par, c, iy], s_r.at[par, c], r_r.at[par, c], row_peers)
        per = LANES // SUB
        for c in range(chunks):
            drain(rbuf.at[par, c, 0:ny - 1], r_r.at[par, c])
            r = rbuf[par, c, 0]
            for d in range(1, ny):
                r = r + rbuf[par, c, d]
            sl8 = slice(c * CHUNK, (c + 1) * CHUNK)
            r_ref[sl8, :] = r
            t_ref[gu, sl8, :] = a_ref[sl8, :] / r
            for t in range(ctiles):
                block = []
                for s in range(t * per, (t + 1) * per):
                    sl = slice(s * SUB, (s + 1) * SUB)
                    acc = t_ref[ga, sl, :] if c else None
                    for q in range(c * CHUNK, (c + 1) * CHUNK):
                        val = t_ref[q, sl, :] * t_ref[gu, q:q + 1, :]
                        acc = val if acc is None else acc + val
                    if c < chunks - 1:
                        t_ref[ga, sl, :] = acc
                    block.append(acc)
                if c == chunks - 1:
                    line = jnp.sum(jnp.transpose(jnp.concatenate(block, axis=0)), axis=0, keepdims=True)
                    cbuf[par, me, t:t + 1, :] = line * v_ref[t:t + 1, :]
        cbuf[par, me, ctiles:ctiles + 1, :] = jnp.sum(jnp.abs(r_ref[...] - a_ref[...]), axis=0, keepdims=True)
        cbuf[par, me, ctiles + 1:ctiles + 2, :] = err0_ref[...]
        send(cbuf.at[par, me, 0:ctiles + 2], s_c.at[par], r_c.at[par], col_peers)
        f_ref[...] = f_ref[...] + jnp.log2(t_ref[gu, 0:tiles, :])
        spread(gc_ref[...], gl)
        lax.fori_loop(0, tiles // group, rebuild, 0)
        for c in range(chunks):
            drain(rbuf.at[par, c, 0:ny - 1], s_r.at[par, c])
        drain(cbuf.at[par, 0:ng - 1, 0:ctiles + 2], r_c.at[par])
        got = cbuf[par, 0]
        for d in range(1, ng):
            got = got + cbuf[par, d]
        old = got[0:ctiles]
        bv = b_ref[...]
        v = bv / old
        v_ref[...] = v
        gc_ref[...] = gc_ref[...] + jnp.log2(v)
        ebuf[iy, pl.ds(k, 1), :] = jnp.sum(jnp.abs(old - bv), axis=0, keepdims=True)
        errs_ref[pl.ds(k, 1), :] = got[ctiles:ctiles + 1]
        errs_ref[0:1, :] = got[ctiles + 1:ctiles + 2]
        drain(cbuf.at[par, 0:ng - 1, 0:ctiles + 2], s_c.at[par])
        return carry

    lax.fori_loop(1, ITERS, iteration, 0)
    send(ebuf.at[iy], s_e, r_e, row_peers)
    f_out[...] = (f_ref[...] + rho_ref[...]) * (1.0 / SCALE)
    g_out[...] = (gc_ref[...] + cap_ref[...]) * (1.0 / SCALE)
    drain(ebuf.at[0:ny - 1], r_e)
    drain(ebuf.at[0:ny - 1], s_e)
    ce = ebuf[0]
    for d in range(1, ny):
        ce = ce + ebuf[d]
    errs_ref[pad:2 * pad, :] = ce
    both = jnp.sum(jnp.transpose(errs_ref[...]), axis=0, keepdims=True)
    e_out[0:1, :] = both[:, 0:ITERS]
    e_out[1:2, :] = both[:, pad:pad + ITERS]


def on_device(row_embed, col_embed, row_mass, col_mass):
    rows, width = row_embed.shape
    cols = col_embed.shape[0]
    nx, nz, ny = lax.axis_size("gx"), lax.axis_size("gz"), lax.axis_size("gy")
    ng = nx * nz
    tiles, ctiles = rows // LANES, cols // LANES
    chunks = tiles // CHUNK
    pad = -(-ITERS // 8) * 8
    crow0 = -(-(2 * ctiles + 1) // 8) * 8
    crow = -(-(ctiles + 2) // 8) * 8
    vm = lambda *s: pltpu.VMEM(s, F32)
    dma = pltpu.SemaphoreType.DMA
    f, g, e = pl.pallas_call(
        functools.partial(kernel, nx, nz, ny),
        out_shape=(jax.ShapeDtypeStruct((tiles, LANES), F32),
                   jax.ShapeDtypeStruct((ctiles, LANES), F32),
                   jax.ShapeDtypeStruct((2, ITERS), F32)),
        in_specs=[pl.BlockSpec(memory_space=pl.ANY)] * 4,
        out_specs=[pl.BlockSpec(memory_space=pltpu.VMEM)] * 3,
        scratch_shapes=[
            vm(tiles, cols, LANES), vm(tiles + 4, cols, LANES),
            vm(tiles, LANES), vm(tiles, LANES), vm(tiles, LANES), vm(tiles, LANES),
            vm(ctiles, LANES), vm(ctiles, LANES), vm(ctiles, LANES),
            vm(1, LANES), vm(LANES, LANES), vm(CHUNK, LANES), vm(ctiles, LANES),
            vm(tiles, LANES), vm(chunks, ny, 3 * CHUNK, LANES), vm(2, chunks, ny, CHUNK, LANES),
            vm(ng, crow0, LANES), vm(2, ng, crow, LANES), vm(ny, pad, LANES),
            pltpu.VMEM((rows, width), row_embed.dtype), pltpu.VMEM((cols, width), col_embed.dtype),
            vm(tiles, LANES), vm(ctiles, LANES), dma((2,)), dma, dma((2,)), dma((chunks,)), dma((chunks,)), dma((2, chunks)), dma((2, chunks)), dma, dma, dma((2,)), dma((2,)), dma, dma,
        ],
        compiler_params=pltpu.CompilerParams(
            collective_id=0, has_side_effects=True, vmem_limit_bytes=67043328),
    )(row_embed, col_embed, row_mass.reshape(tiles, LANES), col_mass.reshape(ctiles, LANES))
    return f.reshape(rows), g.reshape(cols), e.T


def solution(mesh):
    in_specs = (P(("gx", "gz"), None), P("gy", None), P(("gx", "gz")), P("gy"))
    out_specs = (P(("gx", "gz")), P("gy"), P())
    return jax.shard_map(
        on_device, mesh=mesh, in_specs=in_specs, out_specs=out_specs, check_vma=False
    )
```

time: 81.5 us -> 77.1 us (0.946)
  Pallas kernels: 78 us -> 73.6 us
    pallas_call x1, Pallas kernels: 78 us -> 73.6 us  [on_device(): pl.pallas_call(functools.partial(kernel, nx, nz, ny), out_shape=(jax.Shap...]
where the time goes in v1:
time: 77.1 us; the launch traced here: 76.8 us
  Pallas kernels  73.6 us (95%)
  local copies, waits for them, and re-layouts  2.53 us (3%)
    pallas_call x1, Pallas kernels, on_device(): pl.pallas_call(functools.partial(kernel, nx, nz, ny), out_shape=(jax.Shap...  73.6 us
    unnamed x7, local copies, waits for them, and re-layouts  2.53 us

profile of v1, /device:TPU:0, one launch (start us, length us, event | category | flops | bytes accessed | tf_op | source)
XLA Modules:
  0.0 76.8 jit_solution(17984473783541796971)
XLA Ops:
  0.6 73.6 %shard_map.67 = (f32[32,128]{1,0:T(8,128)}, f32[4,128]{1,0:T(4,128)}, f32[2,10]{1,0:T(2,128)}) custom-call(bf16[4096,128]{1,0:T(8,128)(2,1)} %x_hbm.1, bf16[512,128]{1,0:T(8,128)(2,1)} %y_hbm.1, f32[32,128]{1,0:T(8,128)} %bitcast.5, f32[4,128]{1,0:T(4,128)} %bitcast.7), custom_call_target="tpu_custom_call" | custom-call | tf_op jit(solution)/shard_map/pallas_call | solution.py:349
  74.2 0.0 copy-start
  74.2 1.3 %copy.10 = f32[4096]{0:T(1024)} copy(f32[4096]{0:T(1024)} %bitcast.6) | data formatting | bytes 32768
  75.6 0.0 copy-done
  75.6 0.0 copy-start.1
  75.6 0.6 copy.11
  76.2 0.1 copy-done.1
  76.2 0.6 copy.12
Async XLA Ops:
  74.2 1.3 %copy-start = (f32[4,128]{1,0:T(4,128)S(1)}, f32[4,128]{1,0:T(4,128)}, u32[]{:S(2)}) copy-start(f32[4,128]{1,0:T(4,128)} %get-tuple-element.7) | copy-start | bytes 6148
  75.6 0.6 copy-start.1

commit v2 on v1

--- a/solution.py
+++ b/solution.py
@@ -41,20 +41,20 @@
     def row_peer(d):
         return {"gy": lax.rem(iy + d, ny)}
 
+    y_copy = pltpu.make_async_copy(y_hbm, y_ref, s_y)
+    y_copy.start()
+    first = tiles // CHUNK // 2 * CHUNK * LANES
+    cuts = (slice(0, first), slice(first, rows))
+    x_copies = [pltpu.make_async_copy(x_hbm.at[cut], x_ref.at[cut], s_x.at[h]) for h, cut in enumerate(cuts)]
+    m_copies = [pltpu.make_async_copy(cm_hbm, cm_ref, s_m.at[0]), pltpu.make_async_copy(rm_hbm, rm_ref, s_m.at[1])]
+    for copy in x_copies + m_copies:
+        copy.start()
+
     barrier = pltpu.get_barrier_semaphore()
     for d in range(1, ng):
         pl.semaphore_signal(barrier, inc=1, device_id=col_peer(d), device_id_type=MESH)
     for d in range(1, ny):
         pl.semaphore_signal(barrier, inc=1, device_id=row_peer(d), device_id_type=MESH)
-
-    y_copy = pltpu.make_async_copy(y_hbm, y_ref, s_y)
-    y_copy.start()
-    half = rows // 2
-    x_copies = [pltpu.make_async_copy(x_hbm.at[pl.ds(h * half, half)], x_ref.at[pl.ds(h * half, half)], s_x.at[h])
-                for h in range(2)]
-    m_copies = [pltpu.make_async_copy(cm_hbm, cm_ref, s_m.at[0]), pltpu.make_async_copy(rm_hbm, rm_ref, s_m.at[1])]
-    for copy in x_copies + m_copies:
-        copy.start()
 
     def send(buf, ssem, rsem, peers):
         for peer in peers:
@@ -125,50 +125,52 @@
     for c in range(chunks):
         rbuf0[c, iy, 2 * CHUNK:3 * CHUNK, :] = csum
 
-    def build(i, carry):
-        xb = x_ref[pl.ds(pl.multiple_of(i * group * LANES, group * LANES), group * LANES), :]
-        prod = lax.dot_general(y_ref[...], xb, nt, preferred_element_type=F32) * factor
-        for q in range(group):
-            m_ref[i * group + q] = prod[:, q * LANES:(q + 1) * LANES]
+    def product(i):
+        xb = x_ref[i * group * LANES:(i + 1) * group * LANES, :]
+        prod = lax.dot_general(y_ref[...], xb, nt, preferred_element_type=F32)
         tops = [None] * group
         for s in range(nsub):
             sl = slice(s * SUB, (s + 1) * SUB)
             gv = t_ref[gb, sl, :]
             for q in range(group):
-                part = fold(m_ref[i * group + q, sl, :] + gv, jnp.maximum)
+                val = prod[sl, q * LANES:(q + 1) * LANES] * factor + gv
+                m_ref[i * group + q, sl, :] = val
+                part = fold(val, jnp.maximum)
                 tops[q] = part if tops[q] is None else jnp.maximum(tops[q], part)
-        tops = [jnp.max(top, axis=0, keepdims=True) for top in tops]
-        tots = [jnp.zeros((8, LANES), F32) for q in range(group)]
-        for s in range(nsub):
-            sl = slice(s * SUB, (s + 1) * SUB)
-            gv = t_ref[gb, sl, :]
+        return [jnp.max(top, axis=0, keepdims=True) for top in tops]
+
+    def row_sums(i, tops):
+        tots = [None] * group
+        for s in range(nsub):
+            sl = slice(s * SUB, (s + 1) * SUB)
             for q in range(group):
-                val = jnp.exp2((m_ref[i * group + q, sl, :] + gv) - tops[q])
-                tots[q] = tots[q] + fold(val, jnp.add)
-        c = i * group // CHUNK
+                part = fold(jnp.exp2(m_ref[i * group + q, sl, :] - tops[q]), jnp.add)
+                tots[q] = part if tots[q] is None else tots[q] + part
+        c, at = divmod(i * group, CHUNK)
         for q in range(group):
-            at = lax.rem(i * group, CHUNK) + q
-            rbuf0[c, iy, pl.ds(at, 1), :] = tops[q]
-            rbuf0[c, iy, pl.ds(CHUNK + at, 1), :] = jnp.sum(tots[q], axis=0, keepdims=True)
-        return carry
+            rbuf0[c, iy, at + q:at + q + 1, :] = tops[q]
+            rbuf0[c, iy, CHUNK + at + q:CHUNK + at + q + 1, :] = jnp.sum(tots[q], axis=0, keepdims=True)
 
     steps = tiles // group
+    per = CHUNK // group
+    half = chunks // 2 * per
     x_copies[0].wait()
-    lax.fori_loop(0, steps // 2, build, 0)
-    x_copies[1].wait()
-    lax.fori_loop(steps // 2, steps, build, 0)
-    pl.semaphore_wait(barrier, (ng - 1) + (ny - 1))
-
-    def push0(c, carry):
-        send(rbuf0.at[c, iy], s_r0.at[c], r_r0.at[c], row_peers)
-        return carry
-
-    lax.fori_loop(0, chunks, push0, 0)
-    t_ref[ga] = jnp.full((cols, LANES), -jnp.inf, F32)
-
-    def colmax(c, carry):
+    tops = product(0)
+    for i in range(steps):
+        if i + 1 == half:
+            x_copies[1].wait()
+        ahead = product(i + 1) if i + 1 < steps else None
+        row_sums(i, tops)
+        tops = ahead
+        if i + 1 == half:
+            pl.semaphore_wait(barrier, (ng - 1) + (ny - 1))
+            for c in range(half // per):
+                send(rbuf0.at[c, iy], s_r0.at[c], r_r0.at[c], row_peers)
+        elif i + 1 > half and (i + 1) % per == 0:
+            c = i // per
+            send(rbuf0.at[c, iy], s_r0.at[c], r_r0.at[c], row_peers)
+    for c in range(chunks):
         drain(rbuf0.at[c, 0:ny - 1], r_r0.at[c])
-        drain(rbuf0.at[c, 0:ny - 1], s_r0.at[c])
         top = rbuf0[c, 0, 0:CHUNK, :]
         for d in range(1, ny):
             top = jnp.maximum(top, rbuf0[c, d, 0:CHUNK, :])
@@ -176,38 +178,32 @@
         for d in range(ny):
             tot = tot + rbuf0[c, d, CHUNK:2 * CHUNK, :] * jnp.exp2(rbuf0[c, d, 0:CHUNK, :] - top)
         lse = top + jnp.log2(tot)
-        sl8 = pl.ds(pl.multiple_of(c * CHUNK, CHUNK), CHUNK)
+        sl8 = slice(c * CHUNK, (c + 1) * CHUNK)
         lse_ref[sl8, :] = lse
         fv = jnp.log2(rm_ref[sl8, :]) - lse
         f_ref[sl8, :] = fv
-        w_ref[...] = fv
-        for s in range(nsub):
-            sl = slice(s * SUB, (s + 1) * SUB)
-            acc = t_ref[ga, sl, :]
-            for q in range(CHUNK):
-                acc = jnp.maximum(acc, m_ref[c * CHUNK + q, sl, :] + w_ref[q:q + 1, :])
+        t_ref[gu, sl8, :] = fv
+        for s in range(nsub):
+            sl = slice(s * SUB, (s + 1) * SUB)
+            acc = t_ref[ga, sl, :] if c else None
+            for q in range(c * CHUNK, (c + 1) * CHUNK):
+                val = m_ref[q, sl, :] + t_ref[gu, q:q + 1, :]
+                acc = val if acc is None else jnp.maximum(acc, val)
             t_ref[ga, sl, :] = acc
-        return carry
-
-    lax.fori_loop(0, chunks, colmax, 0)
+    for c in range(chunks):
+        drain(rbuf0.at[c, 0:ny - 1], s_r0.at[c])
     ctop = squeeze(jnp.max)
     spread(ctop, gb)
-    t_ref[ga] = jnp.zeros((cols, LANES), F32)
-
-    def colsum(c, carry):
-        w_ref[...] = f_ref[pl.ds(pl.multiple_of(c * CHUNK, CHUNK), CHUNK), :]
-        for s in range(nsub):
-            sl = slice(s * SUB, (s + 1) * SUB)
-            acc = t_ref[ga, sl, :]
+    for c in range(chunks):
+        for s in range(nsub):
+            sl = slice(s * SUB, (s + 1) * SUB)
+            acc = t_ref[ga, sl, :] if c else None
             gv = t_ref[gb, sl, :]
-            for q in range(CHUNK):
-                val = jnp.exp2((m_ref[c * CHUNK + q, sl, :] + w_ref[q:q + 1, :]) - gv)
-                t_ref[c * CHUNK + q, sl, :] = val
-                acc = acc + val
+            for q in range(c * CHUNK, (c + 1) * CHUNK):
+                val = jnp.exp2((m_ref[q, sl, :] + t_ref[gu, q:q + 1, :]) - gv)
+                t_ref[q, sl, :] = val
+                acc = val if acc is None else acc + val
             t_ref[ga, sl, :] = acc
-        return carry
-
-    lax.fori_loop(0, chunks, colsum, 0)
     ctot = rbuf0[0, 0, 2 * CHUNK:2 * CHUNK + 1, :]
     for d in range(1, ny):
         ctot = ctot + rbuf0[0, d, 2 * CHUNK:2 * CHUNK + 1, :]
@@ -246,8 +242,9 @@
     f_ref[...] = f_ref[...] - lrt
     err0_ref[...] = jnp.sum(jnp.abs(jnp.exp2(lse_ref[...] - rho_ref[...]) - a), axis=0, keepdims=True)
     clse = top + jnp.log2(tot) - lrt
-    gc_ref[...] = jnp.log2(bv) - clse
-    ebuf[iy, 0:1, :] = jnp.sum(jnp.abs(jnp.exp2(clse - cap_ref[...]) - bv), axis=0, keepdims=True)
+    kap = cap_ref[...]
+    gc_ref[...] = jnp.log2(bv) - clse - kap
+    ebuf[iy, 0:1, :] = jnp.sum(jnp.abs(jnp.exp2(clse) - bv), axis=0, keepdims=True)
     drain(cbuf0.at[0:ng - 1], s_c0)
 
     def rebuild(i, carry):
@@ -273,7 +270,7 @@
             for q in range(CHUNK):
                 rbuf[par, c, iy, q:q + 1, :] = jnp.sum(tots[q], axis=0, keepdims=True)
             send(rbuf.at[par, c, iy], s_r.at[par, c], r_r.at[par, c], row_peers)
-        per = LANES // SUB
+        subs = LANES // SUB
         for c in range(chunks):
             drain(rbuf.at[par, c, 0:ny - 1], r_r.at[par, c])
             r = rbuf[par, c, 0]
@@ -284,7 +281,7 @@
             t_ref[gu, sl8, :] = a_ref[sl8, :] / r
             for t in range(ctiles):
                 block = []
-                for s in range(t * per, (t + 1) * per):
+                for s in range(t * subs, (t + 1) * subs):
                     sl = slice(s * SUB, (s + 1) * SUB)
                     acc = t_ref[ga, sl, :] if c else None
                     for q in range(c * CHUNK, (c + 1) * CHUNK):
@@ -300,7 +297,7 @@
         cbuf[par, me, ctiles + 1:ctiles + 2, :] = err0_ref[...]
         send(cbuf.at[par, me, 0:ctiles + 2], s_c.at[par], r_c.at[par], col_peers)
         f_ref[...] = f_ref[...] + jnp.log2(t_ref[gu, 0:tiles, :])
-        spread(gc_ref[...], gl)
+        spread(gc_ref[...] + cap_ref[...], gl)
         lax.fori_loop(0, tiles // group, rebuild, 0)
         for c in range(chunks):
             drain(rbuf.at[par, c, 0:ny - 1], s_r.at[par, c])
@@ -332,6 +329,15 @@
     both = jnp.sum(jnp.transpose(errs_ref[...]), axis=0, keepdims=True)
     e_out[0:1, :] = both[:, 0:ITERS]
     e_out[1:2, :] = both[:, pad:pad + ITERS]
+
+
+def hand_on(f, g, e, f_out, g_out, e_out, sem):
+    copies = [pltpu.make_async_copy(src, dst, sem.at[n])
+              for n, (src, dst) in enumerate(((f, f_out), (g, g_out), (e, e_out)))]
+    for copy in copies:
+        copy.start()
+    for copy in copies:
+        copy.wait()
 
 
 def on_device(row_embed, col_embed, row_mass, col_mass):
@@ -366,6 +372,13 @@
         compiler_params=pltpu.CompilerParams(
             collective_id=0, has_side_effects=True, vmem_limit_bytes=67043328),
     )(row_embed, col_embed, row_mass.reshape(tiles, LANES), col_mass.reshape(ctiles, LANES))
+    f, g, e = pl.pallas_call(
+        hand_on,
+        out_shape=tuple(jax.ShapeDtypeStruct(v.shape, F32) for v in (f, g, e)),
+        in_specs=[pl.BlockSpec(memory_space=pl.ANY)] * 3,
+        out_specs=[pl.BlockSpec(memory_space=pl.ANY)] * 3,
+        scratch_shapes=[dma((3,))],
+    )(f, g, e)
     return f.reshape(rows), g.reshape(cols), e.T
 
 

time: 77.1 us -> 74.9 us (0.971)
  local copies, waits for them, and re-layouts: 2.53 us -> 0 us
    unnamed x7 -> x0, local copies, waits for them, and re-layouts: 2.53 us -> none
    pallas_call x0 -> x1, Pallas kernels: none -> 1.72 us  [on_device(): pl.pallas_call(hand_on, out_shape=tuple((jax.ShapeDtypeStruct(v.shape, F3...]
    pallas_call x1, Pallas kernels: 73.6 us -> 72.4 us  [on_device(): pl.pallas_call(functools.partial(kernel, nx, nz, ny), out_shape=(jax.Shap...]
where the time goes in v2:
time: 74.9 us; the launch traced here: 74.7 us
  Pallas kernels  74.1 us (99%)
    pallas_call x1, Pallas kernels, on_device(): pl.pallas_call(functools.partial(kernel, nx, nz, ny), out_shape=(jax.Shap...  72.4 us
    pallas_call x1, Pallas kernels, on_device(): pl.pallas_call(hand_on, out_shape=tuple((jax.ShapeDtypeStruct(v.shape, F3...  1.72 us

profile of v2, /device:TPU:0, one launch (start us, length us, event | category | flops | bytes accessed | tf_op | source)
XLA Modules:
  0.0 74.7 jit_solution(16018006297966872611)
XLA Ops:
  0.6 72.4 %shard_map.67 = (f32[32,128]{1,0:T(8,128)}, f32[4,128]{1,0:T(4,128)}, f32[2,10]{1,0:T(2,128)}) custom-call(bf16[4096,128]{1,0:T(8,128)(2,1)} %x_hbm.1, bf16[512,128]{1,0:T(8,128)(2,1)} %y_hbm.1, f32[32,128]{1,0:T(8,128)} %bitcast.5, f32[4,128]{1,0:T(4,128)} %bitcast.6), custom_call_target="tpu_custom_call" | custom-call | tf_op jit(solution)/shard_map/pallas_call | solution.py:355
  73.0 1.7 %shard_map.68 = (f32[32,128]{1,0:T(8,128)}, f32[4,128]{1,0:T(4,128)}, f32[2,10]{1,0:T(2,128)}) custom-call(f32[32,128]{1,0:T(8,128)} %get-tuple-element.9.f, f32[4,128]{1,0:T(4,128)} %get-tuple-element.10.g, f32[2,10]{1,0:T(2,128)} %get-tuple-element.11.e), custom_call_target="tpu_custom_call" | custom-call | tf_op jit(solution)/shard_map/pallas_call | solution.py:375

commit v3 on v2

--- a/solution.py
+++ b/solution.py
@@ -18,10 +18,15 @@
 MESH = pl.DeviceIdType.MESH
 
 
+def row_pieces(tiles):
+    cuts = list(range(0, tiles, CHUNK // 2)) + [tiles]
+    return list(zip(cuts[:-1], cuts[1:]))
+
+
 def kernel(nx, nz, ny, x_hbm, y_hbm, rm_hbm, cm_hbm, f_out, g_out, e_out,
            m_ref, t_ref, f_ref, r_ref, a_ref, rho_ref, cap_ref, gc_ref, b_ref,
-           err0_ref, errs_ref, w_ref, v_ref, lse_ref, rbuf0, rbuf, cbuf0, cbuf, ebuf,
-           x_ref, y_ref, rm_ref, cm_ref, s_x, s_y, s_m, s_r0, r_r0, s_r, r_r, s_c0, r_c0, s_c, r_c, s_e, r_e):
+           err0_ref, le_ref, errs_ref, w_ref, v_ref, lse_ref, rbuf0, rbuf, cbuf0, cbuf, ebuf, obuf,
+           x_ref, y_ref, rm_ref, cm_ref, s_x, s_y, s_m, s_r0, r_r0, s_r, r_r, s_c0, r_c0, s_c, r_c, s_e, r_e, s_o, r_o):
     rows, width = x_ref.shape
     cols = y_ref.shape[0]
     tiles = rows // LANES
@@ -29,6 +34,7 @@
     chunks = tiles // CHUNK
     nsub = cols // SUB
     gb, ga, gl, gu = range(tiles, tiles + 4)
+    pieces = row_pieces(tiles)
     ix, iz, iy = lax.axis_index("gx"), lax.axis_index("gz"), lax.axis_index("gy")
     ng = nx * nz
     me = ix * nz + iz
@@ -54,7 +60,9 @@
     for d in range(1, ng):
         pl.semaphore_signal(barrier, inc=1, device_id=col_peer(d), device_id_type=MESH)
     for d in range(1, ny):
-        pl.semaphore_signal(barrier, inc=1, device_id=row_peer(d), device_id_type=MESH)
+        for j in range(ng):
+            peer = {**(col_peer(j) if j else {"gx": ix, "gz": iz}), **row_peer(d)}
+            pl.semaphore_signal(barrier, inc=1, device_id=peer, device_id_type=MESH)
 
     def send(buf, ssem, rsem, peers):
         for peer in peers:
@@ -83,6 +91,7 @@
     else:
         col_peers = [far_peer(i) for i in range(ng - 1, 0, -1)]
     row_peers = [row_peer(d) for d in range(1, ny)]
+    cross_peers = [{**peer, **across} for across in row_peers for peer in col_peers + [{"gx": ix, "gz": iz}]]
 
     def spread(compact, slot):
         for t in range(ctiles):
@@ -113,17 +122,13 @@
         return (parts[0] + parts[1]) * (SCALE / width)
 
     y_copy.wait()
+    x_copies[0].wait()
     yv = y_ref[...]
     yf = yv.astype(F32)
     ysq = row_norm(yf)
     kap = jnp.concatenate([ysq[0:1, t * LANES:(t + 1) * LANES] for t in range(ctiles)], axis=0)
     cap_ref[...] = kap
     spread(-kap, gb)
-    for copy in m_copies:
-        copy.wait()
-    csum = jnp.broadcast_to(jnp.sum(cm_ref[...], axis=0, keepdims=True), (CHUNK, LANES))
-    for c in range(chunks):
-        rbuf0[c, iy, 2 * CHUNK:3 * CHUNK, :] = csum
 
     def product(i):
         xb = x_ref[i * group * LANES:(i + 1) * group * LANES, :]
@@ -154,16 +159,20 @@
     steps = tiles // group
     per = CHUNK // group
     half = chunks // 2 * per
-    x_copies[0].wait()
     tops = product(0)
     for i in range(steps):
         if i + 1 == half:
             x_copies[1].wait()
+            for copy in m_copies:
+                copy.wait()
+            for c in range(chunks):
+                rbuf0[c, iy, 2 * CHUNK:2 * CHUNK + 1, :] = jnp.sum(cm_ref[...], axis=0, keepdims=True)
+                rbuf0[c, iy, 2 * CHUNK + 1:2 * CHUNK + 1 + ctiles, :] = cm_ref[...]
         ahead = product(i + 1) if i + 1 < steps else None
         row_sums(i, tops)
         tops = ahead
         if i + 1 == half:
-            pl.semaphore_wait(barrier, (ng - 1) + (ny - 1))
+            pl.semaphore_wait(barrier, ng * ny - 1)
             for c in range(half // per):
                 send(rbuf0.at[c, iy], s_r0.at[c], r_r0.at[c], row_peers)
         elif i + 1 > half and (i + 1) % per == 0:
@@ -188,6 +197,7 @@
             acc = t_ref[ga, sl, :] if c else None
             for q in range(c * CHUNK, (c + 1) * CHUNK):
                 val = m_ref[q, sl, :] + t_ref[gu, q:q + 1, :]
+                t_ref[q, sl, :] = val
                 acc = val if acc is None else jnp.maximum(acc, val)
             t_ref[ga, sl, :] = acc
     for c in range(chunks):
@@ -200,7 +210,7 @@
             acc = t_ref[ga, sl, :] if c else None
             gv = t_ref[gb, sl, :]
             for q in range(c * CHUNK, (c + 1) * CHUNK):
-                val = jnp.exp2((m_ref[q, sl, :] + t_ref[gu, q:q + 1, :]) - gv)
+                val = jnp.exp2(t_ref[q, sl, :] - gv)
                 t_ref[q, sl, :] = val
                 acc = val if acc is None else acc + val
             t_ref[ga, sl, :] = acc
@@ -244,7 +254,7 @@
     clse = top + jnp.log2(tot) - lrt
     kap = cap_ref[...]
     gc_ref[...] = jnp.log2(bv) - clse - kap
-    ebuf[iy, 0:1, :] = jnp.sum(jnp.abs(jnp.exp2(clse) - bv), axis=0, keepdims=True)
+    le_ref[...] = jnp.sum(jnp.abs(jnp.exp2(clse) - bv), axis=0, keepdims=True)
     drain(cbuf0.at[0:ng - 1], s_c0)
 
     def rebuild(i, carry):
@@ -259,48 +269,64 @@
     def iteration(k, carry):
         par = lax.rem(k, 2)
         spread(v_ref[...], gb)
-        for c in range(chunks):
-            tots = [None] * CHUNK
+        for n, (lo, hi) in enumerate(pieces):
+            tots = [None] * (hi - lo)
             for s in range(nsub):
                 sl = slice(s * SUB, (s + 1) * SUB)
                 gv = t_ref[gb, sl, :]
-                for q in range(CHUNK):
-                    part = fold(t_ref[c * CHUNK + q, sl, :] * gv, jnp.add)
-                    tots[q] = part if tots[q] is None else tots[q] + part
-            for q in range(CHUNK):
-                rbuf[par, c, iy, q:q + 1, :] = jnp.sum(tots[q], axis=0, keepdims=True)
-            send(rbuf.at[par, c, iy], s_r.at[par, c], r_r.at[par, c], row_peers)
+                for q in range(lo, hi):
+                    part = fold(t_ref[q, sl, :] * gv, jnp.add)
+                    tots[q - lo] = part if tots[q - lo] is None else tots[q - lo] + part
+            for q in range(lo, hi):
+                rbuf[par, iy, q:q + 1, :] = jnp.sum(tots[q - lo], axis=0, keepdims=True)
+            send(rbuf.at[par, iy, lo:hi], s_r.at[par, n], r_r.at[par, n], row_peers)
         subs = LANES // SUB
-        for c in range(chunks):
-            drain(rbuf.at[par, c, 0:ny - 1], r_r.at[par, c])
-            r = rbuf[par, c, 0]
+        def receive(n):
+            lo, hi = pieces[n]
+            drain(rbuf.at[par, 0:ny - 1, lo:hi], r_r.at[par, n])
+            r = rbuf[par, 0, lo:hi, :]
             for d in range(1, ny):
-                r = r + rbuf[par, c, d]
-            sl8 = slice(c * CHUNK, (c + 1) * CHUNK)
-            r_ref[sl8, :] = r
-            t_ref[gu, sl8, :] = a_ref[sl8, :] / r
+                r = r + rbuf[par, d, lo:hi, :]
+            r_ref[lo:hi, :] = r
+            t_ref[gu, lo:hi, :] = a_ref[lo:hi, :] / r
+
+        receive(0)
+        for n, (lo, hi) in enumerate(pieces):
+            last = n == len(pieces) - 1
             for t in range(ctiles):
+                if t == ctiles - 1 and not last:
+                    receive(n + 1)
                 block = []
                 for s in range(t * subs, (t + 1) * subs):
                     sl = slice(s * SUB, (s + 1) * SUB)
-                    acc = t_ref[ga, sl, :] if c else None
-                    for q in range(c * CHUNK, (c + 1) * CHUNK):
+                    acc = t_ref[ga, sl, :] if n else None
+                    for q in range(lo, hi):
                         val = t_ref[q, sl, :] * t_ref[gu, q:q + 1, :]
                         acc = val if acc is None else acc + val
-                    if c < chunks - 1:
+                    if not last:
                         t_ref[ga, sl, :] = acc
                     block.append(acc)
-                if c == chunks - 1:
+                if last:
                     line = jnp.sum(jnp.transpose(jnp.concatenate(block, axis=0)), axis=0, keepdims=True)
                     cbuf[par, me, t:t + 1, :] = line * v_ref[t:t + 1, :]
         cbuf[par, me, ctiles:ctiles + 1, :] = jnp.sum(jnp.abs(r_ref[...] - a_ref[...]), axis=0, keepdims=True)
         cbuf[par, me, ctiles + 1:ctiles + 2, :] = err0_ref[...]
         send(cbuf.at[par, me, 0:ctiles + 2], s_c.at[par], r_c.at[par], col_peers)
+        ebuf[iy, pl.ds(k - 1, 1), :] = le_ref[...]
+
+        @pl.when(k == ITERS - 1)
+        def _():
+            for peer in cross_peers:
+                pltpu.make_async_remote_copy(
+                    src_ref=cbuf.at[par, me, 0:ctiles], dst_ref=obuf.at[iy, me, 0:ctiles],
+                    send_sem=s_o, recv_sem=r_o, device_id=peer, device_id_type=MESH).start()
+            send(ebuf.at[iy], s_e, r_e, row_peers)
+
         f_ref[...] = f_ref[...] + jnp.log2(t_ref[gu, 0:tiles, :])
         spread(gc_ref[...] + cap_ref[...], gl)
         lax.fori_loop(0, tiles // group, rebuild, 0)
-        for c in range(chunks):
-            drain(rbuf.at[par, c, 0:ny - 1], s_r.at[par, c])
+        for n, (lo, hi) in enumerate(pieces):
+            drain(rbuf.at[par, 0:ny - 1, lo:hi], s_r.at[par, n])
         drain(cbuf.at[par, 0:ng - 1, 0:ctiles + 2], r_c.at[par])
         got = cbuf[par, 0]
         for d in range(1, ng):
@@ -310,22 +336,32 @@
         v = bv / old
         v_ref[...] = v
         gc_ref[...] = gc_ref[...] + jnp.log2(v)
-        ebuf[iy, pl.ds(k, 1), :] = jnp.sum(jnp.abs(old - bv), axis=0, keepdims=True)
+        le_ref[...] = jnp.sum(jnp.abs(old - bv), axis=0, keepdims=True)
         errs_ref[pl.ds(k, 1), :] = got[ctiles:ctiles + 1]
         errs_ref[0:1, :] = got[ctiles + 1:ctiles + 2]
         drain(cbuf.at[par, 0:ng - 1, 0:ctiles + 2], s_c.at[par])
         return carry
 
     lax.fori_loop(1, ITERS, iteration, 0)
-    send(ebuf.at[iy], s_e, r_e, row_peers)
     f_out[...] = (f_ref[...] + rho_ref[...]) * (1.0 / SCALE)
     g_out[...] = (gc_ref[...] + cap_ref[...]) * (1.0 / SCALE)
     drain(ebuf.at[0:ny - 1], r_e)
     drain(ebuf.at[0:ny - 1], s_e)
+    drain(obuf.at[0:ny - 1, 0:ng, 0:ctiles], r_o)
     ce = ebuf[0]
     for d in range(1, ny):
         ce = ce + ebuf[d]
     errs_ref[pad:2 * pad, :] = ce
+    tail = le_ref[...]
+    for d in range(1, ny):
+        other = lax.rem(iy + d, ny)
+        seen = obuf[other, 0, 0:ctiles, :]
+        for c in range(1, ng):
+            seen = seen + obuf[other, c, 0:ctiles, :]
+        bo = rbuf0[0, other, 2 * CHUNK + 1:2 * CHUNK + 1 + ctiles, :] / jnp.sum(ctot, axis=1, keepdims=True)
+        tail = tail + jnp.sum(jnp.abs(seen - bo), axis=0, keepdims=True)
+    errs_ref[pad + ITERS - 1:pad + ITERS, :] = tail
+    drain(obuf.at[0:ny - 1, 0:ng, 0:ctiles], s_o)
     both = jnp.sum(jnp.transpose(errs_ref[...]), axis=0, keepdims=True)
     e_out[0:1, :] = both[:, 0:ITERS]
     e_out[1:2, :] = both[:, pad:pad + ITERS]
@@ -347,6 +383,7 @@
     ng = nx * nz
     tiles, ctiles = rows // LANES, cols // LANES
     chunks = tiles // CHUNK
+    npieces = len(row_pieces(tiles))
     pad = -(-ITERS // 8) * 8
     crow0 = -(-(2 * ctiles + 1) // 8) * 8
     crow = -(-(ctiles + 2) // 8) * 8
@@ -363,11 +400,11 @@
             vm(tiles, cols, LANES), vm(tiles + 4, cols, LANES),
             vm(tiles, LANES), vm(tiles, LANES), vm(tiles, LANES), vm(tiles, LANES),
             vm(ctiles, LANES), vm(ctiles, LANES), vm(ctiles, LANES),
-            vm(1, LANES), vm(LANES, LANES), vm(CHUNK, LANES), vm(ctiles, LANES),
-            vm(tiles, LANES), vm(chunks, ny, 3 * CHUNK, LANES), vm(2, chunks, ny, CHUNK, LANES),
-            vm(ng, crow0, LANES), vm(2, ng, crow, LANES), vm(ny, pad, LANES),
+            vm(1, LANES), vm(1, LANES), vm(LANES, LANES), vm(CHUNK, LANES), vm(ctiles, LANES),
+            vm(tiles, LANES), vm(chunks, ny, 3 * CHUNK, LANES), vm(2, ny, tiles, LANES),
+            vm(ng, crow0, LANES), vm(2, ng, crow, LANES), vm(ny, pad, LANES), vm(ny, ng, ctiles, LANES),
             pltpu.VMEM((rows, width), row_embed.dtype), pltpu.VMEM((cols, width), col_embed.dtype),
-            vm(tiles, LANES), vm(ctiles, LANES), dma((2,)), dma, dma((2,)), dma((chunks,)), dma((chunks,)), dma((2, chunks)), dma((2, chunks)), dma, dma, dma((2,)), dma((2,)), dma, dma,
+            vm(tiles, LANES), vm(ctiles, LANES), dma((2,)), dma, dma((2,)), dma((chunks,)), dma((chunks,)), dma((2, npieces)), dma((2, npieces)), dma, dma, dma((2,)), dma((2,)), dma, dma, dma, dma,
         ],
         compiler_params=pltpu.CompilerParams(
             collective_id=0, has_side_effects=True, vmem_limit_bytes=67043328),

time: 74.9 us -> 73.8 us (0.985)
  Pallas kernels: 74.1 us -> 73 us
    pallas_call x1, Pallas kernels: 72.4 us -> 71.3 us  [on_device(): pl.pallas_call(functools.partial(kernel, nx, nz, ny), out_shape=(jax.Shap...]
where the time goes in v3:
time: 73.8 us; the launch traced here: 73.7 us
  Pallas kernels  73 us (99%)
    pallas_call x1, Pallas kernels, on_device(): pl.pallas_call(functools.partial(kernel, nx, nz, ny), out_shape=(jax.Shap...  71.3 us
    pallas_call x1, Pallas kernels, on_device(): pl.pallas_call(hand_on, out_shape=tuple((jax.ShapeDtypeStruct(v.shape, F3...  1.72 us

profile of v3, /device:TPU:0, one launch (start us, length us, event | category | flops | bytes accessed | tf_op | source)
XLA Modules:
  0.0 73.7 jit_solution(9648260934441850202)
XLA Ops:
  0.6 71.3 %shard_map.67 = (f32[32,128]{1,0:T(8,128)}, f32[4,128]{1,0:T(4,128)}, f32[2,10]{1,0:T(2,128)}) custom-call(bf16[4096,128]{1,0:T(8,128)(2,1)} %x_hbm.1, bf16[512,128]{1,0:T(8,128)(2,1)} %y_hbm.1, f32[32,128]{1,0:T(8,128)} %bitcast.5, f32[4,128]{1,0:T(4,128)} %bitcast.6), custom_call_target="tpu_custom_call" | custom-call | tf_op jit(solution)/shard_map/pallas_call | solution.py:392
  72.0 1.7 %shard_map.68 = (f32[32,128]{1,0:T(8,128)}, f32[4,128]{1,0:T(4,128)}, f32[2,10]{1,0:T(2,128)}) custom-call(f32[32,128]{1,0:T(8,128)} %get-tuple-element.9.f, f32[4,128]{1,0:T(4,128)} %get-tuple-element.10.g, f32[2,10]{1,0:T(2,128)} %get-tuple-element.11.e), custom_call_target="tpu_custom_call" | custom-call | tf_op jit(solution)/shard_map/pallas_call | solution.py:412
